TPU v7x, 32 devices: a whole 2x2x4 slice. The times are simulated.
32 devices in a mesh: pix: 8 (over z, y), rep: 4 (over x, core).
Axes of the slice: x: 2, y: 2, z: 4, core: 2. Of those that a mesh axis runs over, the one named last changes fastest.
Arguments:
- interferograms: float32 [256, 131072], P(('pix', 'rep')), may hold values from -6 to 6
- epoch_pairs: int32 [2, 256], replicated, may hold values from 0 to 63, as said below
- los: float32 [3, 131072], P(None, ('pix', 'rep')), may hold values from 0.3 to 1
- patch_place: int32 [2, 4096], replicated, may hold values from 0 to 255, as said below
- patch_depth: int32 [4096], replicated, may hold values from 0 to 7
Outputs:
- predicted: float32 [64, 131072], P(None, ('pix', 'rep'))
- slip: float32 [64, 4096], P(None, ('pix', 'rep'))
Inputs may be any that keep to these rules, and one draw needn't show every extreme that they name: `epoch_pairs`: row 0 holds an interferogram's earlier epoch and row 1 its later one; the two always differ. `patch_place`: row 0 is an east cell below 256; row 1 is a north cell below 32.
All inputs are finite; a program needn't handle non-finite values.
Results may differ from a plain program's by a relative error of at most 0.0037.
Values may be sent and summed in bfloat16 or wider, within the bound.
A program may use at most 64 MiB of HBM per device.

v0:
```python
import jax
import jax.numpy as jnp
from jax import lax
from jax.sharding import PartitionSpec as P

NEP = 64
IMG_W = 1024


pixel_step = 0.1
patch_step = 0.4
damping = 0.5
depth_base = 0.5
depth_step = 0.25


def sbas_inverse(epoch_pairs, epochs_count):
    epochs = lax.iota(jnp.int32, epochs_count)
    design = (epochs[None, :] == epoch_pairs[1][:, None]).astype(jnp.float32) - (
        epochs[None, :] == epoch_pairs[0][:, None]
    ).astype(jnp.float32)
    normal = jnp.dot(design.T, design, precision=lax.Precision.HIGHEST) + damping * jnp.eye(
        epochs_count, dtype=jnp.float32
    )
    factor = jnp.linalg.cholesky(normal)
    return jax.scipy.linalg.cho_solve((factor, True), design.T)


def green_tile(pixel, los_rows, patch_place, patch_depth):
    column = (pixel % IMG_W).astype(jnp.float32)
    line = (pixel // IMG_W).astype(jnp.float32)
    xpos = (column + 0.5) * pixel_step
    ypos = (line + 0.5) * pixel_step
    patch_x = (patch_place[0].astype(jnp.float32) + 0.5) * patch_step
    patch_y = (patch_place[1].astype(jnp.float32) + 0.5) * patch_step
    patch_z = depth_base + depth_step * patch_depth.astype(jnp.float32)
    delta_x = xpos[:, None] - patch_x[None, :]
    delta_y = ypos[:, None] - patch_y[None, :]
    delta_z = patch_z[None, :]
    dist_sq = delta_x * delta_x + delta_y * delta_y + delta_z * delta_z
    toward = (
        los_rows[0][:, None] * delta_x
        + los_rows[1][:, None] * delta_y
        + los_rows[2][:, None] * delta_z
    )
    return (delta_z * toward / (dist_sq * jnp.sqrt(dist_sq))).astype(jnp.bfloat16)


def on_device(interferograms, epoch_pairs, los, patch_place, patch_depth):
    devices = lax.axis_size(("pix", "rep"))
    ifg_dev, total = interferograms.shape
    pix_dev = total // devices
    epochs_count = NEP
    npatch = patch_depth.shape[0]
    own = npatch // devices
    pseudo = sbas_inverse(epoch_pairs, epochs_count)
    pieces = interferograms.reshape(ifg_dev, devices, pix_dev)
    series = jnp.dot(
        pseudo,
        lax.all_to_all(pieces, ("pix", "rep"), split_axis=1, concat_axis=0, tiled=True)[:, 0, :],
        precision=lax.Precision.HIGHEST,
        preferred_element_type=jnp.float32,
    )
    anchor = lax.axis_index(("pix", "rep")) * pix_dev
    width = min(512, pix_dev)
    count = pix_dev // width

    def tile_at(index):
        start = index * width
        pixel = anchor + start + lax.iota(jnp.int32, width)
        los_rows = lax.dynamic_slice_in_dim(los, start, width, 1)
        return (green_tile(pixel, los_rows, patch_place, patch_depth), start)

    def first_step(index, carry):
        rhs, bound = carry
        tile, start = tile_at(index)
        resid = lax.dynamic_slice_in_dim(series, start, width, 1).astype(jnp.bfloat16)
        rhs = rhs + jnp.dot(resid, tile, preferred_element_type=jnp.float32)
        magnitude = jnp.abs(tile)
        weight = jnp.sum(magnitude.astype(jnp.float32), axis=1).astype(jnp.bfloat16)
        bound = bound + jnp.dot(weight[None, :], magnitude, preferred_element_type=jnp.float32)
        return (rhs, bound)

    zero_rhs = jnp.zeros((epochs_count, npatch), jnp.float32)
    zero_bound = jnp.zeros((1, npatch), jnp.float32)
    rhs, bound = lax.fori_loop(0, count, first_step, (zero_rhs, zero_bound))
    rhs_all, bound_all = lax.psum((rhs, bound), ("pix", "rep"))
    slip_all = rhs_all / bound_all
    sweep_slip_half = slip_all.astype(jnp.bfloat16)

    def sweep_step(index, rhs_now):
        tile, start = tile_at(index)
        guess = lax.dot_general(
            sweep_slip_half, tile, (((1,), (1,)), ((), ())), preferred_element_type=jnp.float32
        )
        resid = (lax.dynamic_slice_in_dim(series, start, width, 1) - guess).astype(jnp.bfloat16)
        return rhs_now + jnp.dot(resid, tile, preferred_element_type=jnp.float32)

    rhs = lax.fori_loop(0, count, sweep_step, zero_rhs)
    slip_all = slip_all + lax.psum(rhs, ("pix", "rep")) / bound_all
    slip_half = slip_all.astype(jnp.bfloat16)
    slip_own = lax.dynamic_slice_in_dim(slip_all, lax.axis_index(("pix", "rep")) * own, own, 1)

    def final_step(index, predicted):
        tile, start = tile_at(index)
        block = lax.dot_general(
            slip_half, tile, (((1,), (1,)), ((), ())), preferred_element_type=jnp.float32
        )
        return lax.dynamic_update_slice_in_dim(predicted, block, start, 1)

    predicted = lax.fori_loop(0, count, final_step, jnp.zeros((epochs_count, pix_dev), jnp.float32))
    return (predicted, slip_own)


def solution(mesh):
    placed = (P(("pix", "rep"), None), P(), P(None, ("pix", "rep")), P(), P())
    return jax.shard_map(
        on_device,
        mesh=mesh,
        in_specs=placed,
        out_specs=(P(None, ("pix", "rep")), P(None, ("pix", "rep"))),
        check_vma=False,
    )
```

profile of v0, /device:TPU:0, one launch (start us, length us, event | category | flops | bytes accessed | tf_op | source)
XLA Modules:
  0.0 731.8 jit_solution(1607313868562399574)
XLA Ops:
  7.2 7.5 %all-to-all-start = ((f32[8,32,4096]{2,0,1:T(8,128)}), f32[8,32,4096]{2,0,1:T(8,128)}, u32[]{:S(2)}, u32[]{:S(2)}) async-start(f32[8,32,4096]{2,0,1:T(8,128)} %bitcast.110), calls=%async_computation | async-start | bytes 8388608 | tf_op jit(solution)/shard_map/all_to_all | solution.py:60
  28.2 80.2 %all-to-all-done = f32[8,32,4096]{2,0,1:T(8,128)} async-done(((f32[8,32,4096]{2,0,1:T(8,128)}), f32[8,32,4096]{2,0,1:T(8,128)}, u32[]{:S(2)}, u32[]{:S(2)}) %all-to-all-start) | async-done | bytes 4194336 | tf_op jit(solution)/shard_map/all_to_all | solution.py:60
  114.1 168.4 %while.53 = (s32[]{:T(128)}, f32[64,4096]{1,0:T(8,128)S(1)}, f32[1,4096]{1,0:T(1,128)S(1)}, bf16[64,4096]{1,0:T(8,128)(2,1)S(1)}, f32[1,4096]{1,0:T(1,128)S(1)},...) while((s32[]{:T(128)}, f32[64,4096]{1,0:T(8,128)S(1)}, ...), condition=%wide.region_4.5_spmd.clone, body=%wide.region_2.4_spmd.clone.sunk | while | flops 373867008 | bytes 2590974 | solution.py:86
  115.3 6.6 convolution_add_fusion.6
  121.9 6.8 abs_reduce_fusion.2
  136.3 6.6 convolution_add_fusion.6
  142.8 6.8 abs_reduce_fusion.2
  157.3 6.6 convolution_add_fusion.6
  163.8 6.8 abs_reduce_fusion.2
  178.2 6.6 convolution_add_fusion.6
  184.8 6.8 abs_reduce_fusion.2
  199.2 6.6 convolution_add_fusion.6
  205.8 6.8 abs_reduce_fusion.2
  220.2 6.6 convolution_add_fusion.6
  226.8 6.8 abs_reduce_fusion.2
  241.2 6.6 convolution_add_fusion.6
  247.7 6.8 abs_reduce_fusion.2
  262.1 6.6 convolution_add_fusion.6
  268.7 6.8 abs_reduce_fusion.2
  283.6 38.4 %psum.22 = f32[4096]{0:T(1024)S(1)} all-reduce(f32[4096]{0:T(1024)S(1)} %bitcast.147), channel_id=1, replica_groups=mesh['pix'=8,'rep'=4] {'pix','rep'}, use_global_device_ids=true, to_apply=%region_6.7 | all-reduce | flops 4096 | bytes 32768 | tf_op jit(solution)/shard_map/psum | solution.py:87
  322.0 92.1 %all-reduce.3.cloned.1.call-done = f32[64,4096]{1,0:T(8,128)} async-done(((f32[64,4096]{1,0:T(8,128)}), f32[64,4096]{1,0:T(8,128)}) %all-reduce.3.cloned.1.call-update) | async-done | bytes 1048592 | tf_op jit(solution)/shard_map/psum | solution.py:87
  415.4 117.2 %while.54 = (s32[]{:T(128)}, f32[64,4096]{1,0:T(8,128)S(1)}, f32[64,4096]{1,0:T(8,128)}, f32[1,4096]{1,0:T(1,128)S(1)}, f32[3,4096]{1,0:T(4,128)}, /*index=5*/s3...) while((s32[]{:T(128)}, f32[64,4096]{1,0:T(8,128)S(1)}, ...), condition=%wide.region_8.9_spmd.clone, body=%wide.region_7.8_spmd.clone.sunk | while | flops 600417280 | bytes 3068157 | solution.py:99
  416.4 13.6 %convolution_add_fusion.8 = f32[64,4096]{1,0:T(8,128)S(1)} fusion(f32[4096]{0:T(1024)S(1)} %mul.1511, f32[512]{0:T(512)S(1)} %bitcast.143, f32[4096]{0:T(1024)S(1)} %bitcast.128, f32[512]{0:T(512)S(1)} %get-tuple-element.1055, f32[512]{0:T(512)S(1)} %bitcast.142, f32[4096]{0:T(1024)S(1)} %bitcast.129, f32[512]{0:T(512)S(1)} %get-tuple-element.1058, ...), kind=kOutput, calls=%fused_computation.86.clone.1 | convolution fusion | flops 600375296 | bytes 2904069 | tf_op jit(solution)/shard_map/while/body/eval_jaxpr/dot_general | solution.py:97
  431.0 13.6 %convolution_add_fusion.8 = f32[64,4096]{1,0:T(8,128)S(1)} fusion(f32[4096]{0:T(1024)S(1)} %mul.1511, f32[512]{0:T(512)S(1)} %bitcast.143, f32[4096]{0:T(1024)S(1)} %bitcast.128, f32[512]{0:T(512)S(1)} %get-tuple-element.1055, f32[512]{0:T(512)S(1)} %bitcast.142, f32[4096]{0:T(1024)S(1)} %bitcast.129, f32[512]{0:T(512)S(1)} %get-tuple-element.1058, ...), kind=kOutput, calls=%fused_computation.86.clone.1 | convolution fusion | flops 600375296 | bytes 2904069 | tf_op jit(solution)/shard_map/while/body/eval_jaxpr/dot_general | solution.py:97
  445.6 13.6 %convolution_add_fusion.8 = f32[64,4096]{1,0:T(8,128)S(1)} fusion(f32[4096]{0:T(1024)S(1)} %mul.1511, f32[512]{0:T(512)S(1)} %bitcast.143, f32[4096]{0:T(1024)S(1)} %bitcast.128, f32[512]{0:T(512)S(1)} %get-tuple-element.1055, f32[512]{0:T(512)S(1)} %bitcast.142, f32[4096]{0:T(1024)S(1)} %bitcast.129, f32[512]{0:T(512)S(1)} %get-tuple-element.1058, ...), kind=kOutput, calls=%fused_computation.86.clone.1 | convolution fusion | flops 600375296 | bytes 2904069 | tf_op jit(solution)/shard_map/while/body/eval_jaxpr/dot_general | solution.py:97
  460.3 13.6 %convolution_add_fusion.8 = f32[64,4096]{1,0:T(8,128)S(1)} fusion(f32[4096]{0:T(1024)S(1)} %mul.1511, f32[512]{0:T(512)S(1)} %bitcast.143, f32[4096]{0:T(1024)S(1)} %bitcast.128, f32[512]{0:T(512)S(1)} %get-tuple-element.1055, f32[512]{0:T(512)S(1)} %bitcast.142, f32[4096]{0:T(1024)S(1)} %bitcast.129, f32[512]{0:T(512)S(1)} %get-tuple-element.1058, ...), kind=kOutput, calls=%fused_computation.86.clone.1 | convolution fusion | flops 600375296 | bytes 2904069 | tf_op jit(solution)/shard_map/while/body/eval_jaxpr/dot_general | solution.py:97
  474.9 13.6 %convolution_add_fusion.8 = f32[64,4096]{1,0:T(8,128)S(1)} fusion(f32[4096]{0:T(1024)S(1)} %mul.1511, f32[512]{0:T(512)S(1)} %bitcast.143, f32[4096]{0:T(1024)S(1)} %bitcast.128, f32[512]{0:T(512)S(1)} %get-tuple-element.1055, f32[512]{0:T(512)S(1)} %bitcast.142, f32[4096]{0:T(1024)S(1)} %bitcast.129, f32[512]{0:T(512)S(1)} %get-tuple-element.1058, ...), kind=kOutput, calls=%fused_computation.86.clone.1 | convolution fusion | flops 600375296 | bytes 2904069 | tf_op jit(solution)/shard_map/while/body/eval_jaxpr/dot_general | solution.py:97
  489.5 13.6 %convolution_add_fusion.8 = f32[64,4096]{1,0:T(8,128)S(1)} fusion(f32[4096]{0:T(1024)S(1)} %mul.1511, f32[512]{0:T(512)S(1)} %bitcast.143, f32[4096]{0:T(1024)S(1)} %bitcast.128, f32[512]{0:T(512)S(1)} %get-tuple-element.1055, f32[512]{0:T(512)S(1)} %bitcast.142, f32[4096]{0:T(1024)S(1)} %bitcast.129, f32[512]{0:T(512)S(1)} %get-tuple-element.1058, ...), kind=kOutput, calls=%fused_computation.86.clone.1 | convolution fusion | flops 600375296 | bytes 2904069 | tf_op jit(solution)/shard_map/while/body/eval_jaxpr/dot_general | solution.py:97
  504.1 13.6 %convolution_add_fusion.8 = f32[64,4096]{1,0:T(8,128)S(1)} fusion(f32[4096]{0:T(1024)S(1)} %mul.1511, f32[512]{0:T(512)S(1)} %bitcast.143, f32[4096]{0:T(1024)S(1)} %bitcast.128, f32[512]{0:T(512)S(1)} %get-tuple-element.1055, f32[512]{0:T(512)S(1)} %bitcast.142, f32[4096]{0:T(1024)S(1)} %bitcast.129, f32[512]{0:T(512)S(1)} %get-tuple-element.1058, ...), kind=kOutput, calls=%fused_computation.86.clone.1 | convolution fusion | flops 600375296 | bytes 2904069 | tf_op jit(solution)/shard_map/while/body/eval_jaxpr/dot_general | solution.py:97
  518.8 13.6 %convolution_add_fusion.8 = f32[64,4096]{1,0:T(8,128)S(1)} fusion(f32[4096]{0:T(1024)S(1)} %mul.1511, f32[512]{0:T(512)S(1)} %bitcast.143, f32[4096]{0:T(1024)S(1)} %bitcast.128, f32[512]{0:T(512)S(1)} %get-tuple-element.1055, f32[512]{0:T(512)S(1)} %bitcast.142, f32[4096]{0:T(1024)S(1)} %bitcast.129, f32[512]{0:T(512)S(1)} %get-tuple-element.1058, ...), kind=kOutput, calls=%fused_computation.86.clone.1 | convolution fusion | flops 600375296 | bytes 2904069 | tf_op jit(solution)/shard_map/while/body/eval_jaxpr/dot_general | solution.py:97
  533.5 129.8 %all-reduce.5.cloned.1.call-done = f32[64,4096]{1,0:T(8,128)} async-done(((f32[64,4096]{1,0:T(8,128)}), f32[64,4096]{1,0:T(8,128)}) %all-reduce.5.cloned.1.call-update) | async-done | bytes 1048592 | tf_op jit(solution)/shard_map/psum | solution.py:100
  664.8 59.0 %while.52 = (s32[]{:T(128)}, f32[64,4096]{1,0:T(8,128)S(1)}, f32[1,4096]{1,0:T(1,128)S(1)}, f32[3,4096]{1,0:T(4,128)}, s32[]{:T(128)}, /*index=5*/f32[1,4096]{1,...) while((s32[]{:T(128)}, f32[64,4096]{1,0:T(8,128)S(1)}, ...), condition=%wide.region_11.12_spmd, body=%wide.region_10.11_spmd.sunk | while | flops 299934720 | bytes 895211 | solution.py:111
  (185 shorter events, 151.6 us)
Async XLA Ops:
  7.2 7.6 %copy-start.7 = (s32[2,256]{1,0:T(2,128)S(1)}, s32[2,256]{1,0:T(2,128)}, u32[]{:S(2)}) copy-start(s32[2,256]{1,0:T(2,128)} %param.12) | copy-start | bytes 6148
  7.2 20.3 %copy-start.6 = (s32[4096]{0:T(1024)S(1)}, s32[4096]{0:T(1024)}, u32[]{:S(2)}) copy-start(s32[4096]{0:T(1024)} %param.15) | copy-start | bytes 49156
  7.2 20.9 %copy-start.5 = (s32[2,4096]{1,0:T(2,128)S(1)}, s32[2,4096]{1,0:T(2,128)}, u32[]{:S(2)}) copy-start(s32[2,4096]{1,0:T(2,128)} %param.14) | copy-start | bytes 98308
  7.2 101.2 %all-to-all-start = ((f32[8,32,4096]{2,0,1:T(8,128)}), f32[8,32,4096]{2,0,1:T(8,128)}, u32[]{:S(2)}, u32[]{:S(2)}) async-start(f32[8,32,4096]{2,0,1:T(8,128)} %bitcast.110), calls=%async_computation | async-start | bytes 8388608 | tf_op jit(solution)/shard_map/all_to_all | solution.py:60
  14.7 399.4 %all-reduce.3.cloned.1.call-start = ((), (), s32[]{:S(2)}) async-start(), calls=%async_computation.1 | async-start | bytes 2097152 | tf_op jit(solution)/shard_map/psum | solution.py:87
  282.5 1.0 copy-start.1
  283.5 379.8 %all-reduce.5.cloned.1.call-start = ((), (), s32[]{:S(2)}) async-start(), calls=%async_computation.2 | async-start | bytes 2097152 | tf_op jit(solution)/shard_map/psum | solution.py:100
  322.0 93.4 %copy-start.4 = (f32[4096]{0:T(1024)}, f32[4096]{0:T(1024)S(1)}, u32[]{:S(2)}) copy-start(f32[4096]{0:T(1024)S(1)} %psum.22) | copy-start | bytes 49156
  415.4 248.0 %copy-start = (f32[64,4096]{1,0:T(8,128)S(1)}, f32[64,4096]{1,0:T(8,128)}, u32[]{:S(2)}) copy-start(f32[64,4096]{1,0:T(8,128)} %all-reduce.3.cloned.1.call-done) | copy-start | bytes 3145732
  532.5 1.0 copy-start.2
  723.8 1.0 copy-start.3
Sparse Core Ops, SparseCore 0:
  283.7 130.3 all-reduce.2
  533.7 129.6 all-reduce.4
where the time goes:
time: 743 us; the launch traced here: 732 us
  waiting for transfers between devices  302 us (41%)
  matrix products  271 us (36%)
  other arithmetic  71.6 us (10%)
  blocking collectives  38.4 us (5%)
  local copies, waits for them, and re-layouts  24.6 us (3%)
  between operations  14.5 us (2%)
  starting transfers between devices  7.54 us (1%)
    psum x1, waiting for transfers between devices, on_device(): slip_all = slip_all + lax.psum(rhs, ('pix', 'rep')) / bound_all  130 us
    dot_general x8, matrix products, sweep_step(): return rhs_now + jnp.dot(resid, tile, preferred_element_type=jnp.float32)  109 us
    psum x1, waiting for transfers between devices, on_device(): rhs_all, bound_all = lax.psum((rhs, bound), ('pix', 'rep'))  92.1 us
    all_to_all x1, waiting for transfers between devices, on_device(): lax.all_to_all(pieces, ('pix', 'rep'), split_axis=1, concat_axis=0, tiled...  80.2 us
    reduce_sum x8, other arithmetic, first_step(): weight = jnp.sum(magnitude.astype(jnp.float32), axis=1).astype(jnp.bfloat16)  54.8 us
    dot_general x8, matrix products, first_step(): rhs = rhs + jnp.dot(resid, tile, preferred_element_type=jnp.float32)  52.5 us
    dot_general x8, matrix products, first_step(): jnp.dot(weight[None, :], magnitude, preferred_element_type=jnp.float32)  52.4 us
    dot_general x8, matrix products, final_step(): lax.dot_general(slip_half, tile, (((1,), (1,)), ((), ())), preferred_elem...  50.8 us
  transfers between devices with their start and end apart: 3, of which 3 were waited for; matrix products, arithmetic and copies ran while one was open for 2% of the time, Pallas kernels for 0%

commit v1 on v0

v1 whole, which is shorter than its diff:
```python
import functools

import jax
import jax.numpy as jnp
from jax import lax
from jax.experimental import pallas as pl
from jax.experimental.pallas import tpu as pltpu
from jax.sharding import PartitionSpec as P

NEP = 64
IMG_W = 1024
LANES = 128

pixel_step = 0.1
patch_step = 0.4
damping = 0.5
depth_base = 0.5
depth_step = 0.25

F32 = jnp.float32
BF16 = jnp.bfloat16
NT = (((1,), (1,)), ((), ()))
EXTRA = 16


def kernel(
    cfg,
    pairs_ref,
    pcol_ref,
    prow_ref,
    xs_ref,
    pred_ref,
    slip_ref,
    green,
    wacc,
    got,
    series,
    resid,
    brow,
    send,
    part_a,
    part_b,
    gath_a,
    gath_b,
    full,
    s_x,
    r_x,
    s_p,
    r_pa,
    r_pb,
    s_g,
    r_ga,
    r_gb,
):
    n, reps, npix, npatch, parts, ifg_dev, lines = cfg
    me = lax.axis_index(("pix", "rep"))
    rep_size = lax.axis_size("rep")
    groups = npatch // LANES
    mine = me // reps
    gathered = n // reps

    def ident(d):
        return {"pix": d // rep_size, "rep": d % rep_size}

    def settle(buf, count, sem):
        view = buf.at[pl.ds(0, count)]
        pltpu.make_async_copy(view, view, sem).wait()

    barrier = pltpu.get_barrier_semaphore()

    @pl.loop(1, n)
    def _(k):
        pl.semaphore_signal(
            barrier, inc=1, device_id=ident((me + k) % n), device_id_type=pl.DeviceIdType.MESH
        )

    pl.semaphore_wait(barrier, n - 1)

    @pl.loop(1, n)
    def _(k):
        d = (me + k) % n
        pltpu.make_async_remote_copy(
            src_ref=xs_ref.at[d],
            dst_ref=got.at[me],
            send_sem=s_x,
            recv_sem=r_x.at[0],
            device_id=ident(d),
            device_id_type=pl.DeviceIdType.MESH,
        ).start()

    own_copy = pltpu.make_async_copy(xs_ref.at[me], got.at[me], r_x.at[1])
    own_copy.start()

    strip, wide = 32, 256
    per_line = IMG_W // strip

    for line in range(lines):

        @pl.loop(0, per_line)
        def _(t):
            start = pl.multiple_of(line * IMG_W + t * strip, strip)
            col = pcol_ref[pl.ds(start, strip), :]
            xpos = jnp.broadcast_to(col[:, 0:1], (strip, LANES))
            east = jnp.broadcast_to(col[:, 1:2], (strip, LANES))
            north = jnp.broadcast_to(col[:, 2:3], (strip, LANES))
            upward = jnp.broadcast_to(col[:, 3:4], (strip, LANES))
            total = jnp.zeros((strip, LANES), F32)
            for c in range(npatch // wide):
                halves = []
                for j in range(wide // LANES):
                    at = slice(c * wide + j * LANES, c * wide + (j + 1) * LANES)
                    u = (xpos - prow_ref[0:1, at]) * prow_ref[1:2, at]
                    r2 = u * u + prow_ref[4 + 2 * line : 5 + 2 * line, at]
                    inv = lax.rsqrt(r2)
                    num = east * u + north * prow_ref[3 + 2 * line : 4 + 2 * line, at]
                    num = num + upward * prow_ref[2:3, at]
                    g = num * (inv * inv * inv)
                    total = total + jnp.abs(g)
                    halves.append(g.astype(BF16))
                green[pl.ds(start, strip), c * wide : (c + 1) * wide] = jnp.concatenate(halves, 1)
            wacc[pl.ds(start, strip), :] = total

    weight = lax.dot_general(
        jnp.ones((EXTRA, LANES), F32),
        wacc[...],
        NT,
        precision=lax.Precision.HIGHEST,
        preferred_element_type=F32,
    ).astype(BF16)
    block = 512

    @pl.loop(0, npatch // block)
    def _(b):
        cols = pl.ds(pl.multiple_of(b * block, block), block)
        row = jnp.dot(weight, jnp.abs(green[:, cols]), preferred_element_type=F32)
        brow[:, cols] = row

    rows = parts * n * ifg_dev
    ep = lax.broadcasted_iota(jnp.int32, (NEP, rows), 0)
    later = (ep == pairs_ref[1:2, :]).astype(F32)
    earlier = (ep == pairs_ref[0:1, :]).astype(F32)
    design = later - earlier
    design_half = design.astype(BF16)
    sub = lax.broadcasted_iota(jnp.int32, (NEP, NEP), 0)
    lane = lax.broadcasted_iota(jnp.int32, (NEP, NEP), 1)
    normal = lax.dot_general(design_half, design_half, NT, preferred_element_type=F32) * (1.0 / parts)
    normal = normal + jnp.where(sub == lane, damping, 0.0)

    def sweep(k, m):
        col = jnp.sum(jnp.where(lane == k, m, 0.0), axis=1, keepdims=True)
        row = jnp.sum(jnp.where(sub == k, m, 0.0), axis=0, keepdims=True)
        pivot = jnp.sum(jnp.where(lane[0:1] == k, row, 0.0), axis=1, keepdims=True)
        inv = 1.0 / pivot
        scaled = row * inv
        new = m - col * scaled
        new = jnp.where(lane == k, col * inv, new)
        new = jnp.where(sub == k, scaled, new)
        return jnp.where((sub == k) & (lane == k), -inv, new)

    inverse = -lax.fori_loop(0, NEP, sweep, normal)
    inv_hi = inverse.astype(BF16)
    rest = inverse - inv_hi.astype(F32)
    inv_mid = rest.astype(BF16)
    inv_lo = (rest - inv_mid.astype(F32)).astype(BF16)
    pseudo = (
        jnp.dot(inv_hi, design_half, preferred_element_type=F32)
        + jnp.dot(inv_mid, design_half, preferred_element_type=F32)
        + jnp.dot(inv_lo, design_half, preferred_element_type=F32)
    )
    which = (lax.broadcasted_iota(jnp.int32, (NEP, rows), 1) // ifg_dev) % parts

    settle(got, n - 1, r_x.at[0])
    own_copy.wait()
    settle(got, n - 1, s_x)
    width = npix // parts
    stacked = got[...].reshape(rows, width)
    for h in range(parts):
        keep = jnp.where(which == h, pseudo, 0.0)
        hi = keep.astype(BF16)
        lo = (keep - hi.astype(F32)).astype(BF16)
        piece = jnp.dot(hi, stacked, preferred_element_type=F32)
        piece = piece + jnp.dot(lo, stacked, preferred_element_type=F32)
        series[:, h * width : (h + 1) * width] = piece
        resid[:, h * width : (h + 1) * width] = piece.astype(BF16)

    per_block = block // LANES
    blocks = npatch // block
    first_block = mine // per_block

    def project(part, recv_sem):
        @pl.loop(0, blocks)
        def _(b):
            at = (first_block + 1 + b) % blocks
            cols = pl.ds(pl.multiple_of(at * block, block), block)
            out = jnp.dot(resid[...], green[:, cols], preferred_element_type=F32)
            bound = brow[:, cols]
            high = bound.astype(BF16)
            low = (bound - high.astype(F32)).astype(BF16)
            pick = lax.broadcasted_iota(jnp.int32, (EXTRA, block), 0) == 0
            tail = jnp.where(pick, high.astype(F32), low.astype(F32)).astype(BF16)
            half = out.astype(BF16)
            for j in range(per_block):
                send[at * per_block + j, 0:NEP, :] = half[:, j * LANES : (j + 1) * LANES]
                send[at * per_block + j, NEP : NEP + EXTRA, :] = tail[:, j * LANES : (j + 1) * LANES]
            for j in range(per_block):
                group = at * per_block + j
                for r in range(reps):
                    d = group * reps + r

                    @pl.when(d != me)
                    def _():
                        pltpu.make_async_remote_copy(
                            src_ref=send.at[group],
                            dst_ref=part.at[me],
                            send_sem=s_p,
                            recv_sem=recv_sem,
                            device_id=ident(d),
                            device_id_type=pl.DeviceIdType.MESH,
                        ).start()

        part[me, :, :] = send[mine, :, :]
        settle(part, n - 1, recv_sem)
        settle(part, n - 1, s_p)
        return lax.fori_loop(
            1, n, lambda d, acc: acc + part[d].astype(F32), part[0].astype(F32)
        )

    def share(slip, gath, recv_sem):
        gath[mine, :, :] = slip.astype(BF16)

        @pl.loop(1, gathered)
        def _(k):
            d = (me + k * reps) % n
            pltpu.make_async_remote_copy(
                src_ref=gath.at[mine],
                dst_ref=gath.at[mine],
                send_sem=s_g,
                recv_sem=recv_sem,
                device_id=ident(d),
                device_id_type=pl.DeviceIdType.MESH,
            ).start()

        settle(gath, gathered - 1, recv_sem)
        settle(gath, gathered - 1, s_g)
        for g in range(groups):
            full[:, g * LANES : (g + 1) * LANES] = gath[g]

    tile = 512
    sums = project(part_a, r_pa)
    bound = sums[NEP : NEP + 1] + sums[NEP + 1 : NEP + 2]
    slip = sums[:NEP] / bound
    share(slip, gath_a, r_ga)

    @pl.loop(0, npix // tile)
    def _(t):
        at = pl.ds(pl.multiple_of(t * tile, tile), tile)
        guess = lax.dot_general(full[...], green[at, :], NT, preferred_element_type=F32)
        resid[:, at] = (series[:, at] - guess).astype(BF16)

    sums = project(part_b, r_pb)
    slip = slip + sums[:NEP] / bound
    slip_ref[...] = slip
    share(slip, gath_b, r_gb)

    @pl.loop(0, npix // tile)
    def _(t):
        at = pl.ds(pl.multiple_of(t * tile, tile), tile)
        pred_ref[:, at] = lax.dot_general(full[...], green[at, :], NT, preferred_element_type=F32)


def on_device(interferograms, epoch_pairs, los, patch_place, patch_depth):
    n = lax.axis_size(("pix", "rep"))
    me = lax.axis_index(("pix", "rep"))
    ifg_dev, total = interferograms.shape
    npix = total // n
    npatch = patch_depth.shape[0]
    own = npatch // n
    reps = max(LANES // own, 1)
    parts = max(16 // ifg_dev, 1)
    width = npix // parts
    lines = npix // IMG_W
    rows = parts * n * ifg_dev

    xs = interferograms.astype(BF16).reshape(ifg_dev, n, parts, width)
    xs = xs.transpose(1, 2, 0, 3).reshape(n, parts * ifg_dev, width)
    pairs = jnp.broadcast_to(
        epoch_pairs.reshape(2, n, 1, ifg_dev), (2, n, parts, ifg_dev)
    ).reshape(2, rows)

    column = (lax.iota(jnp.int32, npix) % IMG_W).astype(F32)
    xpos = (column + 0.5) * pixel_step
    pcol = jnp.concatenate([xpos[None], los], 0).T

    line = me * lines + lax.iota(jnp.int32, lines)
    ypos = (line.astype(F32) + 0.5) * pixel_step
    patch_x = (patch_place[0].astype(F32) + 0.5) * patch_step
    patch_y = (patch_place[1].astype(F32) + 0.5) * patch_step
    depth = depth_base + depth_step * patch_depth.astype(F32)
    scale = lax.rsqrt(depth)
    prows = [patch_x, scale, depth * scale]
    for i in range(lines):
        dy = ypos[i] - patch_y
        prows += [dy * scale, dy * dy / depth + depth]
    prow = jnp.stack(prows)

    groups = npatch // LANES
    cfg = (n, reps, npix, npatch, parts, ifg_dev, lines)
    vmem = pl.BlockSpec(memory_space=pltpu.VMEM)
    piece = (NEP + EXTRA, LANES)
    dma = pltpu.SemaphoreType.DMA
    predicted, slip = pl.pallas_call(
        functools.partial(kernel, cfg),
        out_shape=(
            jax.ShapeDtypeStruct((NEP, npix), F32),
            jax.ShapeDtypeStruct((NEP, LANES), F32),
        ),
        in_specs=[vmem, vmem, vmem, pl.BlockSpec(memory_space=pl.ANY)],
        out_specs=(vmem, vmem),
        scratch_shapes=[
            pltpu.VMEM((npix, npatch), BF16),
            pltpu.VMEM((npix, LANES), F32),
            pltpu.VMEM((n, parts * ifg_dev, width), BF16),
            pltpu.VMEM((NEP, npix), F32),
            pltpu.VMEM((NEP, npix), BF16),
            pltpu.VMEM((EXTRA, npatch), F32),
            pltpu.VMEM((groups,) + piece, BF16),
            pltpu.VMEM((n,) + piece, BF16),
            pltpu.VMEM((n,) + piece, BF16),
            pltpu.VMEM((groups, NEP, LANES), BF16),
            pltpu.VMEM((groups, NEP, LANES), BF16),
            pltpu.VMEM((NEP, npatch), BF16),
            dma,
            dma((2,)),
            dma,
            dma,
            dma,
            dma,
            dma,
            dma,
        ],
        compiler_params=pltpu.CompilerParams(
            collective_id=0, has_side_effects=True, vmem_limit_bytes=62 * 1024 * 1024
        ),
    )(pairs, pcol, prow, xs)
    if reps > 1:
        slip = lax.dynamic_slice_in_dim(slip, (me % reps) * own, own, 1)
    return (predicted, slip)


def solution(mesh):
    placed = (P(("pix", "rep"), None), P(), P(None, ("pix", "rep")), P(), P())
    return jax.shard_map(
        on_device,
        mesh=mesh,
        in_specs=placed,
        out_specs=(P(None, ("pix", "rep")), P(None, ("pix", "rep"))),
        check_vma=False,
    )
```

time: 743 us -> 171 us (0.23)
  waiting for transfers between devices: 302 us -> 0 us
  matrix products: 271 us -> 0 us
  Pallas kernels: 0 us -> 149 us
  other arithmetic: 71.6 us -> 8.71 us
  blocking collectives: 38.4 us -> 0 us
  local copies, waits for them, and re-layouts: 24.6 us -> 8.64 us
  between operations: 14.5 us -> 0.7 us
  starting transfers between devices: 7.54 us -> 0 us
    dot_general x34 -> x0, matrix products: 271 us -> none  [the longest x8 109 us: sweep_step(): return rhs_now + jnp.dot(resid, tile, preferred_element_type=jnp.float32)]
    psum x2 -> x0, waiting for transfers between devices: 222 us -> none  [the longest x1 130 us: on_device(): slip_all = slip_all + lax.psum(rhs, ('pix', 'rep')) / bound_all]
    pallas_call x0 -> x1, Pallas kernels: none -> 149 us  [on_device(): pl.pallas_call(functools.partial(kernel, cfg), out_shape=(jax.ShapeDtypeS...]
    all_to_all x1 -> x0, waiting for transfers between devices: 80.2 us -> none  [on_device(): lax.all_to_all(pieces, ('pix', 'rep'), split_axis=1, concat_axis=0, tiled...]
    reduce_sum x8 -> x0, other arithmetic: 54.8 us -> none  [first_step(): weight = jnp.sum(magnitude.astype(jnp.float32), axis=1).astype(jnp.bfloat16)]
    psum x1 -> x0, blocking collectives: 38.4 us -> none  [on_device(): rhs_all, bound_all = lax.psum((rhs, bound), ('pix', 'rep'))]
    slice x25 -> x1, local copies, waits for them, and re-layouts: 21.4 us -> 0.67 us  [on_device(): dy = ypos[i] - patch_y]
    another operation x5 -> x0, other arithmetic: 12.1 us -> none  [the longest x3 6.52 us: sbas_inverse(): factor = jnp.linalg.cholesky(normal)]
  transfers between devices with their start and end apart: 3 -> 0, of which waited for: 3 -> 0; matrix products, arithmetic and copies ran while one was open for 2% -> 0% of each run, Pallas kernels for 0% -> 0%
where the time goes in v1:
time: 171 us; the launch traced here: 167 us
  Pallas kernels  149 us (87%)
  other arithmetic  8.71 us (5%)
  local copies, waits for them, and re-layouts  8.64 us (5%)
    pallas_call x1, Pallas kernels, on_device(): pl.pallas_call(functools.partial(kernel, cfg), out_shape=(jax.ShapeDtypeS...  149 us
    convert_element_type x1, other arithmetic, on_device(): xs = interferograms.astype(BF16).reshape(ifg_dev, n, parts, width)  3.69 us

profile of v1, /device:TPU:0, one launch (start us, length us, event | category | flops | bytes accessed | tf_op | source)
XLA Modules:
  0.0 167.2 jit_solution(8349907023074251284)
XLA Ops:
  0.6 0.7 fusion.9
  1.4 0.8 broadcast_in_dim.8
  2.2 0.7 reshape.59.pairs_ref
  2.9 0.9 pad_maximum_fusion
  3.8 1.4 broadcast_subtract_fusion
  5.2 1.9 %broadcast_subtract_fusion.1 = (f32[1,4096]{1,0:T(1,128)S(1)}, f32[1,4096]{1,0:T(1,128)S(1)}, f32[1,4096]{1,0:T(1,128)S(1)}) fusion(f32[1,4096]{1,0:T(1,128)S(1)} %get-tuple-element.3, f32[]{:T(128)} %bitcast.11, f32[]{:T(128)} %bitcast.7, f32[]{:T(128)} %bitcast.3), kind=kLoop, calls=%fused_computation.13 | loop fusion | flops 12288 | bytes 65548 | tf_op jit(solution)/shard_map/sub | solution.py:302
  7.1 0.7 divide_add_fusion
  7.9 1.6 stack.44.prow_ref
  9.5 2.0 %copy.11 = f32[4,4096]{0,1:T(8,128)} copy(f32[4,4096]{1,0:T(4,128)S(1)} %pad_maximum_fusion) | data formatting | bytes 131072 | tf_op jit(solution)/shard_map/concatenate | solution.py:292
  11.4 3.7 %convert_element_type.32 = bf16[8,131072]{1,0:T(8,128)(2,1)} convert(f32[8,131072]{1,0:T(8,128)} %param.5) | non-fusion elementwise | flops 1048576 | bytes 6291456 | tf_op jit(solution)/shard_map/convert_element_type | solution.py:284
  15.1 149.2 %shard_map.68 = (f32[64,4096]{1,0:T(8,128)}, f32[64,128]{1,0:T(8,128)}) custom-call(s32[2,512]{1,0:T(2,128)} %reshape.59.pairs_ref, f32[4096,4]{1,0:T(8,128)} %bitcast.25, f32[11,4096]{1,0:T(8,128)} %stack.44.prow_ref, bf16[32,16,2048]{2,1,0:T(8,128)(2,1)} %bitcast.24), custom_call_target="tpu_custom_call" | custom-call | tf_op jit(solution)/shard_map/pallas_call | solution.py:311
  164.3 0.0 copy-start
  164.3 2.3 %copy.14 = f32[64,4096]{1,0:T(8,128)} copy(f32[64,4096]{1,0:T(8,128)} %get-tuple-element.30) | data formatting | bytes 2097152
  166.6 0.0 copy-done
  166.6 0.6 copy.15
  (3 shorter events, 0.1 us)
Async XLA Ops:
  164.3 2.3 %copy-start = (f32[64,128]{1,0:T(8,128)S(1)}, f32[64,128]{1,0:T(8,128)}, u32[]{:S(2)}) copy-start(f32[64,128]{1,0:T(8,128)} %get-tuple-element.31) | copy-start | bytes 98308

commit v2 on v1

v2 whole, which is shorter than its diff:
```python
import functools

import jax
import jax.numpy as jnp
from jax import lax
from jax.experimental import pallas as pl
from jax.experimental.pallas import tpu as pltpu
from jax.sharding import PartitionSpec as P

NEP = 64
IMG_W = 1024
LANES = 128

pixel_step = 0.1
patch_step = 0.4
damping = 0.5
depth_base = 0.5
depth_step = 0.25

F32 = jnp.float32
BF16 = jnp.bfloat16
NT = (((1,), (1,)), ((), ()))
EXTRA = 16


def kernel(
    cfg,
    pairs_ref,
    los_ref,
    place_ref,
    depth_ref,
    xs_ref,
    pred_ref,
    slip_ref,
    pcol_ref,
    prow_ref,
    mat,
    green,
    wacc,
    got,
    series,
    resid,
    bsend,
    bpart,
    send,
    part_a,
    part_b,
    gath_a,
    gath_b,
    full,
    guess,
    s_x,
    r_x,
    s_b,
    r_b,
    s_p,
    r_pa,
    r_pb,
    s_g,
    r_ga,
    r_gb,
):
    n, reps, npix, npatch, parts, ifg_dev, lines = cfg
    me = lax.axis_index(("pix", "rep"))
    rep_size = lax.axis_size("rep")
    groups = npatch // LANES
    mine = me // reps
    gathered = n // reps

    def ident(d):
        return {"pix": d // rep_size, "rep": d % rep_size}

    def settle(buf, count, sem):
        view = buf.at[pl.ds(0, count)]
        pltpu.make_async_copy(view, view, sem).wait()

    barrier = pltpu.get_barrier_semaphore()

    @pl.loop(1, n)
    def _(k):
        pl.semaphore_signal(
            barrier, inc=1, device_id=ident((me + k) % n), device_id_type=pl.DeviceIdType.MESH
        )

    pl.semaphore_wait(barrier, n - 1)

    @pl.loop(1, n)
    def _(k):
        d = (me + k) % n
        pltpu.make_async_remote_copy(
            src_ref=xs_ref.at[d],
            dst_ref=got.at[me],
            send_sem=s_x,
            recv_sem=r_x.at[0],
            device_id=ident(d),
            device_id_type=pl.DeviceIdType.MESH,
        ).start()

    own_copy = pltpu.make_async_copy(xs_ref.at[me], got.at[me], r_x.at[1])
    own_copy.start()

    patch_x = (place_ref[0:1, :].astype(F32) + 0.5) * patch_step
    patch_y = (place_ref[1:2, :].astype(F32) + 0.5) * patch_step
    depth = depth_base + depth_step * depth_ref[...].astype(F32)
    scale = lax.rsqrt(depth)
    prow_ref[0:1, :] = patch_x
    prow_ref[1:2, :] = scale
    prow_ref[2:3, :] = depth * scale
    for line in range(lines):
        dy = ((me * lines + line).astype(F32) + 0.5) * pixel_step - patch_y
        prow_ref[3 + 2 * line : 4 + 2 * line, :] = dy * scale
        prow_ref[4 + 2 * line : 5 + 2 * line, :] = dy * dy / depth + depth
    pcol_ref[...] = jnp.concatenate([los_ref[...], jnp.zeros((5, npix), F32)], 0).T

    rows = parts * n * ifg_dev
    nifg = n * ifg_dev
    ep = lax.broadcasted_iota(jnp.int32, (NEP, nifg), 0)
    later = (ep == pairs_ref[1:2, :]).astype(F32)
    earlier = (ep == pairs_ref[0:1, :]).astype(F32)
    design = (later - earlier).astype(BF16)
    slot = lax.broadcasted_iota(jnp.int32, (nifg, rows), 1)
    source = slot // (parts * ifg_dev) * ifg_dev + slot % ifg_dev
    spread = (lax.broadcasted_iota(jnp.int32, (nifg, rows), 0) == source).astype(F32).astype(BF16)
    design_half = jnp.dot(design, spread, preferred_element_type=F32).astype(BF16)
    sub = lax.broadcasted_iota(jnp.int32, (NEP, NEP), 0)
    lane = lax.broadcasted_iota(jnp.int32, (NEP, NEP), 1)
    normal = lax.dot_general(design, design, NT, preferred_element_type=F32)
    mat[...] = normal + jnp.where(sub == lane, damping, 0.0)

    def sweep(k):
        m = mat[...]
        col = jnp.sum(jnp.where(lane == k, m, 0.0), axis=1, keepdims=True)
        row = jnp.sum(jnp.where(sub == k, m, 0.0), axis=0, keepdims=True)
        pivot = jnp.sum(jnp.where(lane[0:1] == k, row, 0.0), axis=1, keepdims=True)
        inv = 1.0 / pivot
        scaled = row * inv
        new = m - col * scaled
        new = jnp.where(lane == k, col * inv, new)
        new = jnp.where(sub == k, scaled, new)
        mat[...] = jnp.where((sub == k) & (lane == k), -inv, new)

    strip, wide = 32, 256
    per_line = IMG_W // strip

    for line in range(lines):

        @pl.loop(0, per_line)
        def _(t):
            start = pl.multiple_of(line * IMG_W + t * strip, strip)
            col = pcol_ref[pl.ds(start, strip), :]
            cell = t * strip + lax.broadcasted_iota(jnp.int32, (strip, LANES), 0)
            xpos = (cell.astype(F32) + 0.5) * pixel_step
            east = jnp.broadcast_to(col[:, 0:1], (strip, LANES))
            north = jnp.broadcast_to(col[:, 1:2], (strip, LANES))
            upward = jnp.broadcast_to(col[:, 2:3], (strip, LANES))
            if (line + 1) * per_line <= NEP:
                sweep(line * per_line + t)
            total = jnp.zeros((strip, LANES), F32)
            for c in range(npatch // wide):
                halves = []
                for j in range(wide // LANES):
                    at = slice(c * wide + j * LANES, c * wide + (j + 1) * LANES)
                    u = (xpos - prow_ref[0:1, at]) * prow_ref[1:2, at]
                    r2 = u * u + prow_ref[4 + 2 * line : 5 + 2 * line, at]
                    inv = lax.rsqrt(r2)
                    num = east * u + north * prow_ref[3 + 2 * line : 4 + 2 * line, at]
                    num = num + upward * prow_ref[2:3, at]
                    g = num * (inv * inv * inv)
                    total = total + jnp.abs(g)
                    halves.append(g.astype(BF16))
                green[pl.ds(start, strip), c * wide : (c + 1) * wide] = jnp.concatenate(halves, 1)
            wacc[pl.ds(start, strip), :] = total

    weight = lax.dot_general(
        jnp.ones((EXTRA, LANES), F32),
        wacc[...],
        NT,
        precision=lax.Precision.HIGHEST,
        preferred_element_type=F32,
    ).astype(BF16)
    block = 512

    @pl.loop(0, npatch // block)
    def _(b):
        cols = pl.ds(pl.multiple_of(b * block, block), block)
        row = jnp.dot(weight, jnp.abs(green[:, cols]), preferred_element_type=F32)
        high = row.astype(BF16)
        low = (row - high.astype(F32)).astype(BF16)
        pick = lax.broadcasted_iota(jnp.int32, (EXTRA, block), 0) == 0
        tail = jnp.where(pick, high.astype(F32), low.astype(F32)).astype(BF16)
        for j in range(block // LANES):
            bsend[b * (block // LANES) + j, :, :] = tail[:, j * LANES : (j + 1) * LANES]

    @pl.loop(1, n)
    def _(k):
        d = (me + k) % n
        pltpu.make_async_remote_copy(
            src_ref=bsend.at[d // reps],
            dst_ref=bpart.at[me],
            send_sem=s_b,
            recv_sem=r_b,
            device_id=ident(d),
            device_id_type=pl.DeviceIdType.MESH,
        ).start()

    bpart[me, :, :] = bsend[mine, :, :]

    @pl.loop(min(lines, NEP // per_line) * per_line, NEP)
    def _(k):
        sweep(k)

    inverse = -mat[...]
    inv_hi = inverse.astype(BF16)
    rest = inverse - inv_hi.astype(F32)
    inv_mid = rest.astype(BF16)
    inv_lo = (rest - inv_mid.astype(F32)).astype(BF16)
    pseudo = (
        jnp.dot(inv_hi, design_half, preferred_element_type=F32)
        + jnp.dot(inv_mid, design_half, preferred_element_type=F32)
        + jnp.dot(inv_lo, design_half, preferred_element_type=F32)
    )
    which = (lax.broadcasted_iota(jnp.int32, (NEP, rows), 1) // ifg_dev) % parts

    settle(got, n - 1, r_x.at[0])
    own_copy.wait()
    settle(got, n - 1, s_x)
    width = npix // parts
    stacked = got[...].reshape(rows, width)
    for h in range(parts):
        keep = jnp.where(which == h, pseudo, 0.0)
        hi = keep.astype(BF16)
        lo = (keep - hi.astype(F32)).astype(BF16)
        piece = jnp.dot(hi, stacked, preferred_element_type=F32)
        piece = piece + jnp.dot(lo, stacked, preferred_element_type=F32)
        series[:, h * width : (h + 1) * width] = piece
        resid[:, h * width : (h + 1) * width] = piece.astype(BF16)

    per_block = block // LANES
    blocks = npatch // block
    first_block = mine // per_block

    def project(part, recv_sem, first):
        @pl.loop(0, blocks)
        def _(b):
            at = (first_block + 1 + b) % blocks
            cols = pl.ds(pl.multiple_of(at * block, block), block)
            out = jnp.dot(resid[...], green[:, cols], preferred_element_type=F32)
            half = out.astype(BF16)
            for j in range(per_block):
                send[at * per_block + j, :, :] = half[:, j * LANES : (j + 1) * LANES]
            for j in range(per_block):
                group = at * per_block + j
                for r in range(reps):
                    d = group * reps + r

                    @pl.when(d != me)
                    def _():
                        pltpu.make_async_remote_copy(
                            src_ref=send.at[group],
                            dst_ref=part.at[me],
                            send_sem=s_p,
                            recv_sem=recv_sem,
                            device_id=ident(d),
                            device_id_type=pl.DeviceIdType.MESH,
                        ).start()

        part[me, :, :] = send[mine, :, :]
        settle(part, n - 1, recv_sem)
        settle(part, n - 1, s_p)
        bound = None
        if first:
            settle(bpart, n - 1, r_b)
            settle(bpart, n - 1, s_b)
            both = lax.fori_loop(
                1, n, lambda d, acc: acc + bpart[d].astype(F32), bpart[0].astype(F32)
            )
            bound = both[0:1] + both[1:2]
        total = lax.fori_loop(
            1, n, lambda d, acc: acc + part[d].astype(F32), part[0].astype(F32)
        )
        return total, bound

    tile = 512

    def share(slip, gath, recv_sem, target):
        gath[mine, :, :] = slip.astype(BF16)

        @pl.loop(1, gathered)
        def _(k):
            d = (me + (n - k * reps)) % n
            pltpu.make_async_remote_copy(
                src_ref=gath.at[mine],
                dst_ref=gath.at[mine],
                send_sem=s_g,
                recv_sem=recv_sem.at[first_block],
                device_id=ident(d),
                device_id_type=pl.DeviceIdType.MESH,
            ).start()

        for i in range(blocks):
            at = (first_block + i) % blocks
            settle(gath, per_block - 1 if i == 0 else per_block, recv_sem.at[at])
            for j in range(per_block):
                full[:, j * LANES : (j + 1) * LANES] = gath[at * per_block + j]
            cols = pl.ds(pl.multiple_of(at * block, block), block)

            @pl.loop(0, npix // tile)
            def _(t):
                here = pl.ds(pl.multiple_of(t * tile, tile), tile)
                out = lax.dot_general(full[...], green[here, cols], NT, preferred_element_type=F32)
                if i > 0:
                    out = target[:, here] + out
                target[:, here] = out

        settle(gath, gathered - 1, s_g)

    sums, bound = project(part_a, r_pa, True)
    slip = sums / bound
    share(slip, gath_a, r_ga, guess)
    resid[...] = (series[...] - guess[...]).astype(BF16)
    slip = slip + project(part_b, r_pb, False)[0] / bound
    slip_ref[...] = slip
    share(slip, gath_b, r_gb, pred_ref)


def on_device(interferograms, epoch_pairs, los, patch_place, patch_depth):
    n = lax.axis_size(("pix", "rep"))
    me = lax.axis_index(("pix", "rep"))
    ifg_dev, total = interferograms.shape
    npix = total // n
    npatch = patch_depth.shape[0]
    own = npatch // n
    reps = max(LANES // own, 1)
    parts = max(16 // ifg_dev, 1)
    width = npix // parts
    lines = npix // IMG_W

    xs = interferograms.astype(BF16).reshape(ifg_dev, n, parts, width)
    xs = xs.transpose(1, 2, 0, 3).reshape(n, parts * ifg_dev, width)
    groups = npatch // LANES
    cfg = (n, reps, npix, npatch, parts, ifg_dev, lines)
    vmem = pl.BlockSpec(memory_space=pltpu.VMEM)
    piece = (NEP, LANES)
    block = 512
    dma = pltpu.SemaphoreType.DMA
    predicted, slip = pl.pallas_call(
        functools.partial(kernel, cfg),
        out_shape=(
            jax.ShapeDtypeStruct((NEP, npix), F32),
            jax.ShapeDtypeStruct((NEP, LANES), F32),
        ),
        in_specs=[vmem, vmem, vmem, vmem, pl.BlockSpec(memory_space=pl.ANY)],
        out_specs=(vmem, vmem),
        scratch_shapes=[
            pltpu.VMEM((npix, 8), F32),
            pltpu.VMEM((3 + 2 * lines, npatch), F32),
            pltpu.VMEM((NEP, NEP), F32),
            pltpu.VMEM((npix, npatch), BF16),
            pltpu.VMEM((npix, LANES), F32),
            pltpu.VMEM((n, parts * ifg_dev, width), BF16),
            pltpu.VMEM((NEP, npix), F32),
            pltpu.VMEM((NEP, npix), BF16),
            pltpu.VMEM((groups, EXTRA, LANES), BF16),
            pltpu.VMEM((n, EXTRA, LANES), BF16),
            pltpu.VMEM((groups,) + piece, BF16),
            pltpu.VMEM((n,) + piece, BF16),
            pltpu.VMEM((n,) + piece, BF16),
            pltpu.VMEM((groups, NEP, LANES), BF16),
            pltpu.VMEM((groups, NEP, LANES), BF16),
            pltpu.VMEM((NEP, block), BF16),
            pltpu.VMEM((NEP, npix), F32),
            dma,
            dma((2,)),
            dma,
            dma,
            dma,
            dma,
            dma,
            dma,
            dma((npatch // block,)),
            dma((npatch // block,)),
        ],
        compiler_params=pltpu.CompilerParams(
            collective_id=0, has_side_effects=True, vmem_limit_bytes=62 * 1024 * 1024
        ),
    )(epoch_pairs, los, patch_place, patch_depth[None], xs)
    if reps > 1:
        slip = lax.dynamic_slice_in_dim(slip, (me % reps) * own, own, 1)
    return (predicted, slip)


def solution(mesh):
    placed = (P(("pix", "rep"), None), P(), P(None, ("pix", "rep")), P(), P())
    return jax.shard_map(
        on_device,
        mesh=mesh,
        in_specs=placed,
        out_specs=(P(None, ("pix", "rep")), P(None, ("pix", "rep"))),
        check_vma=False,
    )
```

time: 171 us -> 146 us (0.85); the launches traced: 167 us -> 144 us
  Pallas kernels: 149 us -> 136 us
  local copies, waits for them, and re-layouts: 8.64 us -> 3.64 us
  other arithmetic: 8.71 us -> 3.74 us
    pallas_call x1, Pallas kernels: 149 us -> 136 us  [on_device(): pl.pallas_call(functools.partial(kernel, cfg), out_shape=(jax.ShapeDtypeS...]
    sub x2 -> x0, other arithmetic: 3.37 us -> none  [on_device(): dy = ypos[i] - patch_y]
    concatenate x1 -> x0, local copies, waits for them, and re-layouts: 1.99 us -> none  [on_device(): pcol = jnp.concatenate([xpos[None], los], 0).T]
    unnamed x4 -> x2, local copies, waits for them, and re-layouts: 2.89 us -> 3.64 us
where the time goes in v2:
time: 146 us; the launch traced here: 144 us
  Pallas kernels  136 us (93%)
  other arithmetic  3.74 us (3%)
  local copies, waits for them, and re-layouts  3.64 us (2%)
    pallas_call x1, Pallas kernels, on_device(): pl.pallas_call(functools.partial(kernel, cfg), out_shape=(jax.ShapeDtypeS...  136 us
    convert_element_type x1, other arithmetic, on_device(): xs = interferograms.astype(BF16).reshape(ifg_dev, n, parts, width)  3.74 us
    unnamed x2, local copies, waits for them, and re-layouts  3.64 us

profile of v2, /device:TPU:0, one launch (start us, length us, event | category | flops | bytes accessed | tf_op | source)
XLA Modules:
  0.0 144.4 jit_solution(2026580508555391735)
XLA Ops:
  0.6 3.7 %convert_element_type.3 = bf16[8,131072]{1,0:T(8,128)(2,1)} convert(f32[8,131072]{1,0:T(8,128)} %param.5) | non-fusion elementwise | flops 1048576 | bytes 6291456 | tf_op jit(solution)/shard_map/convert_element_type | solution.py:338
  4.4 136.4 %shard_map.68 = (f32[64,4096]{1,0:T(8,128)}, f32[64,128]{1,0:T(8,128)}) custom-call(s32[2,256]{1,0:T(2,128)} %pairs_ref.1, f32[3,4096]{1,0:T(4,128)} %los_ref.1, s32[2,4096]{1,0:T(2,128)} %place_ref.1, s32[1,4096]{1,0:T(1,128)} %bitcast.7, bf16[32,16,2048]{2,1,0:T(8,128)(2,1)} %bitcast.6), custom_call_target="tpu_custom_call" | custom-call | tf_op jit(solution)/shard_map/pallas_call | solution.py:346
  140.8 2.3 %copy.9 = f32[64,4096]{1,0:T(8,128)} copy(f32[64,4096]{1,0:T(8,128)} %get-tuple-element.4) | data formatting | bytes 2097152
  143.1 1.4 copy.10

commit v3 on v2

--- a/solution.py
+++ b/solution.py
@@ -238,11 +238,12 @@
     per_block = block // LANES
     blocks = npatch // block
     first_block = mine // per_block
+    side = blocks // 2
 
     def project(part, recv_sem, first):
         @pl.loop(0, blocks)
         def _(b):
-            at = (first_block + 1 + b) % blocks
+            at = (first_block // side + 1 + b // side) % 2 * side + (first_block + 1 + b) % side
             cols = pl.ds(pl.multiple_of(at * block, block), block)
             out = jnp.dot(resid[...], green[:, cols], preferred_element_type=F32)
             half = out.astype(BF16)

time: 146 us -> 142 us (0.973)
  Pallas kernels: 136 us -> 134 us
    pallas_call x1, Pallas kernels: 136 us -> 134 us  [on_device(): pl.pallas_call(functools.partial(kernel, cfg), out_shape=(jax.ShapeDtypeS...]
where the time goes in v3:
time: 142 us
  Pallas kernels  134 us (94%)
  other arithmetic  3.74 us (3%)
  local copies, waits for them, and re-layouts  3.64 us (3%)
    pallas_call x1, Pallas kernels, on_device(): pl.pallas_call(functools.partial(kernel, cfg), out_shape=(jax.ShapeDtypeS...  134 us
    convert_element_type x1, other arithmetic, on_device(): xs = interferograms.astype(BF16).reshape(ifg_dev, n, parts, width)  3.74 us
    unnamed x2, local copies, waits for them, and re-layouts  3.64 us

profile of v3, /device:TPU:0, one launch (start us, length us, event | category | flops | bytes accessed | tf_op | source)
XLA Modules:
  0.0 141.6 jit_solution(16060900950329505493)
XLA Ops:
  0.6 3.7 %convert_element_type.3 = bf16[8,131072]{1,0:T(8,128)(2,1)} convert(f32[8,131072]{1,0:T(8,128)} %param.5) | non-fusion elementwise | flops 1048576 | bytes 6291456 | tf_op jit(solution)/shard_map/convert_element_type | solution.py:339
  4.4 133.6 %shard_map.68 = (f32[64,4096]{1,0:T(8,128)}, f32[64,128]{1,0:T(8,128)}) custom-call(s32[2,256]{1,0:T(2,128)} %pairs_ref.1, f32[3,4096]{1,0:T(4,128)} %los_ref.1, s32[2,4096]{1,0:T(2,128)} %place_ref.1, s32[1,4096]{1,0:T(1,128)} %bitcast.7, bf16[32,16,2048]{2,1,0:T(8,128)(2,1)} %bitcast.6), custom_call_target="tpu_custom_call" | custom-call | tf_op jit(solution)/shard_map/pallas_call | solution.py:347
  138.0 2.3 %copy.9 = f32[64,4096]{1,0:T(8,128)} copy(f32[64,4096]{1,0:T(8,128)} %get-tuple-element.4) | data formatting | bytes 2097152
  140.2 1.4 copy.10
